TPU v7x, 128 devices: a whole 4x4x4 slice. The times are simulated.
128 devices in a mesh: tp: 4 (over x), dp: 32 (over z, y, core).
Axes of the slice: x: 4, y: 4, z: 4, core: 2. Of those that a mesh axis runs over, the one named last changes fastest.
Arguments:
- x_saved: bfloat16 [32, 1024, 2048], P('dp', 'tp')
- dy_out: bfloat16 [32, 1024, 2048], P('dp', 'tp')
- ln_params: float32 [4, 2048], replicated
- w_qkv: bfloat16 [2048, 16, 3, 128], P(None, 'tp')
- w_out: bfloat16 [2048, 2048], P('tp')
- w_up: bfloat16 [2048, 8192], P(None, 'tp')
- w_down: bfloat16 [8192, 2048], P('tp')
Outputs:
- output 1: bfloat16 [32, 1024, 2048], P('dp', 'tp')
- output 2: float32 [4, 2048], replicated
- output 3: float32 [2048, 16, 3, 128], P('dp', 'tp')
- output 4: float32 [2048, 2048], P(('tp', 'dp'))
- output 5: float32 [2048, 8192], P('dp', 'tp')
- output 6: float32 [8192, 2048], P(('tp', 'dp'))
All inputs are finite; a program needn't handle non-finite values.
Results may differ from a plain program's by a relative error of at most 0.0110607.
Values are sent between devices in bfloat16 or wider.
A program may use at most 1 GiB of HBM per device.

v0:
```python
import functools

import jax
import jax.numpy as jnp
from jax import lax
from jax.experimental import pallas as pl
from jax.experimental.pallas import tpu as pltpu
from jax.sharding import PartitionSpec as P

NORM_EPS = 1e-5
ROPE_BASE = 10000.0
MESH = pl.DeviceIdType.MESH
PIECES = 12
SLOTS = 6
F32 = jnp.float32
BF16 = jnp.bfloat16


def rope_tables(positions, head_dim):
    half_dim = head_dim // 2
    inv_freq = ROPE_BASE ** (-2.0 * jnp.arange(half_dim, dtype=jnp.float32) / head_dim)
    angles = positions.astype(jnp.float32)[:, None] * inv_freq[None, :]
    return jnp.cos(angles), jnp.sin(angles)


def dot_nn(lhs, rhs):
    return lax.dot_general(lhs, rhs, (((1,), (0,)), ((), ())), preferred_element_type=F32)


def dot_nt(lhs, rhs):
    return lax.dot_general(lhs, rhs, (((1,), (1,)), ((), ())), preferred_element_type=F32)


def dot_tt(lhs, rhs):
    return lax.dot_general(lhs, rhs, (((0,), (0,)), ((), ())), preferred_element_type=F32)


def grads_kernel(gelu_ref, dy_ref, hm_ref, dhid_ref, ha_ref, dproj_ref, ctx_ref, lng_ref,
                 o_down, o_up, o_qkv, o_out, o_ln,
                 a_buf, b_buf, p_buf, d_buf, l1, f1, l2, f2, lnb,
                 a_sem, b_sem, ds, dr, s_l1, r_l1, s_f1, r_f1, s_l2, r_l2, s_f2, r_f2, ln_s, ln_r, credit):
    tp = lax.axis_index('tp')
    dp = lax.axis_index('dp')
    core = lax.rem(dp, 2)
    y = lax.rem(dp // 2, 4)
    z = dp // 8
    partner = {'dp': dp + 1 - 2 * core}

    def dev_y(i):
        return {'dp': z * 8 + i * 2 + core}

    def dev_z(i):
        return {'dp': i * 8 + y * 2 + core}

    def dev_x(i):
        return {'tp': i}

    def ring(i, d):
        return lax.rem(i + d, 4)

    barrier = pltpu.get_barrier_semaphore()
    peers = [partner]
    for d in (1, 2, 3):
        peers += [dev_x(ring(tp, d)), dev_y(ring(y, d)), dev_z(ring(z, d))]
    for peer in peers:
        pl.semaphore_signal(barrier, inc=1, device_id=peer, device_id_type=MESH)

    def load_a(src, slot):
        return pltpu.make_async_copy(src, a_buf.at[slot], a_sem.at[slot])

    def load_b(src, col, slot):
        return pltpu.make_async_copy(src.at[:, pl.ds(pl.multiple_of(col * 512, 512), 512)], b_buf.at[slot], b_sem.at[slot])

    def start_b(p, slot):
        @pl.when(p < 4)
        def _():
            load_b(dy_ref, p, slot).start()

        @pl.when((p >= 4) & (p < 8))
        def _():
            load_b(dhid_ref, p - 4, slot).start()

        @pl.when((p >= 8) & (p < 11))
        def _():
            load_b(dproj_ref, p - 8, slot).start()

        @pl.when(p == 11)
        def _():
            load_b(ctx_ref, 0, slot).start()

    load_a(gelu_ref, 0).start()
    start_b(jnp.int32(0), 0)
    load_a(hm_ref, 1).start()
    pl.semaphore_wait(barrier, len(peers))

    def remote(src, dst, ssem, rsem, device):
        return pltpu.make_async_remote_copy(src_ref=src, dst_ref=dst, send_sem=ssem, recv_sem=rsem, device_id=device, device_id_type=MESH)

    def drain(ref, sem):
        pltpu.make_async_copy(ref, ref, sem).wait()

    def pair_copy(p):
        return remote(p_buf.at[p % 2, :, :, :, 1 - core], d_buf.at[lax.rem(p, SLOTS)], ds.at[p], dr.at[p], partner)

    def blk1(slot, col, i, half):
        rows = pl.ds(32 * half, 32)
        if col == 0:
            return d_buf.at[slot, 0, :, i, rows, :]
        return d_buf.at[slot, 1, i, :, rows, :]

    def blk2(slot, col, i, half):
        rows = pl.ds(32 * half, 32)
        if col == 0:
            return d_buf.at[slot, 0, i, y, rows, :]
        return d_buf.at[slot, 1, z, i, rows, :]

    me1 = (y, z)
    dev1 = (dev_y, dev_z)
    me2 = (z, y)
    dev2 = (dev_z, dev_y)

    def compute(p):
        ps = lax.rem(p, 2)

        @pl.when(p >= 2)
        def _():
            drain(p_buf.at[ps, :, :, :, 0], ds.at[p - 2])

        @pl.when(p < PIECES - 1)
        def _():
            start_b(p + 1, 1 - ps)

        @pl.when((p == 0) | (p == 8))
        def _():
            load_a(gelu_ref, 0).wait()

        @pl.when((p == 4) | (p == 11))
        def _():
            load_a(gelu_ref, 1).wait()

        load_b(dy_ref, 0, ps).wait()

        @pl.when(p < PIECES - 1)
        def _():
            sa = lax.rem(p // 4, 2)

            @pl.loop(0, 8)
            def _(m):
                lhs = a_buf[sa, :, pl.ds(pl.multiple_of(m * 256, 256), 256)]
                tile = dot_tt(lhs, b_buf[ps])
                for i in range(4):
                    for col in range(2):
                        p_buf[ps, col, m // 2, lax.rem(m, 2) * 2 + i // 2, i % 2] = tile[64 * i:64 * i + 64, 256 * col:256 * col + 256]

        @pl.when(p == PIECES - 1)
        def _():
            @pl.loop(0, 8)
            def _(m):
                k = m // 2
                half = lax.rem(m, 2)
                lhs = b_buf[ps]
                rhs = a_buf[1, :, pl.ds(pl.multiple_of(m * 256, 256), 256)]
                tile = dot_tt(lhs, rhs)
                for i in range(32):
                    p_buf[ps, half, i // 8, (i // 2) % 4, i % 2, pl.ds(pl.multiple_of(k * 16, 16), 16), :] = tile[16 * i:16 * i + 16, :]

        @pl.when(p == 3)
        def _():
            load_a(ha_ref, 0).start()

        @pl.when(p == 7)
        def _():
            load_a(dy_ref, 1).start()

        @pl.when(p >= SLOTS)
        def _():
            pl.semaphore_wait(credit, 1)

        pair_copy(p).start()

    def stage_s(q):
        slot = lax.rem(q, SLOTS)
        ps = lax.rem(q, 2)
        drain(d_buf.at[slot], dr.at[q])

        @pl.loop(0, 32)
        def _(i):
            col, zi, yi = i // 16, lax.rem(i // 4, 4), lax.rem(i, 4)
            d_buf[slot, col, zi, yi] = d_buf[slot, col, zi, yi] + p_buf[ps, col, zi, yi, core]

        for col in range(2):
            me, dev = me1[col], dev1[col]
            nxt, opp, prv = ring(me, 1), ring(me, 2), ring(me, 3)
            remote(blk1(slot, col, opp, 0), l1.at[q, col, 0], s_l1.at[q], r_l1.at[q], dev(nxt)).start()
            remote(blk1(slot, col, opp, 1), l1.at[q, col, 1], s_l1.at[q], r_l1.at[q], dev(prv)).start()
        for col in range(2):
            me, dev = me1[col], dev1[col]
            nxt, prv = ring(me, 1), ring(me, 3)
            remote(blk1(slot, col, nxt, 1), f1.at[q, col, 0, 1], s_f1.at[q], r_f1.at[q], dev(nxt)).start()
            remote(blk1(slot, col, prv, 0), f1.at[q, col, 0, 0], s_f1.at[q], r_f1.at[q], dev(prv)).start()

    def stage_l1(q):
        slot = lax.rem(q, SLOTS)
        drain(l1.at[q], r_l1.at[q])
        for col in range(2):
            me, dev = me1[col], dev1[col]
            nxt, prv = ring(me, 1), ring(me, 3)
            for half, to in ((0, nxt), (1, prv)):
                ref = blk1(slot, col, to, half)
                ref[...] = ref[...] + l1[q, col, half]
                remote(ref, f1.at[q, col, 1, half], s_f1.at[q], r_f1.at[q], dev(to)).start()

    def stage_f1(q):
        slot = lax.rem(q, SLOTS)
        drain(f1.at[q], r_f1.at[q])
        for col in range(2):
            for half in range(2):
                ref = blk1(slot, col, me1[col], half)
                ref[...] = ref[...] + (f1[q, col, 0, half] + f1[q, col, 1, half])
        for col in range(2):
            me, dev = me2[col], dev2[col]
            nxt, opp, prv = ring(me, 1), ring(me, 2), ring(me, 3)
            remote(blk2(slot, col, opp, 0), l2.at[q, col, 0], s_l2.at[q], r_l2.at[q], dev(nxt)).start()
            remote(blk2(slot, col, opp, 1), l2.at[q, col, 1], s_l2.at[q], r_l2.at[q], dev(prv)).start()
        for col in range(2):
            me, dev = me2[col], dev2[col]
            nxt, prv = ring(me, 1), ring(me, 3)
            remote(blk2(slot, col, nxt, 1), f2.at[q, col, 0, 1], s_f2.at[q], r_f2.at[q], dev(nxt)).start()
            remote(blk2(slot, col, prv, 0), f2.at[q, col, 0, 0], s_f2.at[q], r_f2.at[q], dev(prv)).start()

    def stage_l2(q):
        slot = lax.rem(q, SLOTS)
        drain(l2.at[q], r_l2.at[q])
        for col in range(2):
            me, dev = me2[col], dev2[col]
            nxt, prv = ring(me, 1), ring(me, 3)
            for half, to in ((0, nxt), (1, prv)):
                ref = blk2(slot, col, to, half)
                ref[...] = ref[...] + l2[q, col, half]
                remote(ref, f2.at[q, col, 1, half], s_f2.at[q], r_f2.at[q], dev(to)).start()

    def stage_f2(q):
        slot = lax.rem(q, SLOTS)
        drain(f2.at[q], r_f2.at[q])
        for col in range(2):
            for half in range(2):
                rows = pl.ds(32 * half, 32)
                val = blk2(slot, col, me2[col], half)[...] + (f2[q, col, 0, half] + f2[q, col, 1, half])
                for out, lo, hi in ((o_down, 0, 4), (o_up, 4, 8), (o_qkv, 8, 11)):
                    @pl.when((q >= lo) & (q < hi))
                    def _():
                        out[rows, pl.ds(pl.multiple_of((q - lo) * 512 + col * 256, 256), 256)] = val

                @pl.when(q == 11)
                def _():
                    for k in range(2):
                        lo = (2 * half + k) * 512 + col * 256
                        o_out[:, lo:lo + 256] = val[16 * k:16 * k + 16, :]
        drain(l1.at[q], s_l1.at[q])
        drain(f1.at[q], s_f1.at[q])
        drain(l2.at[q], s_l2.at[q])
        drain(f2.at[q], s_f2.at[q])

        @pl.when(q < PIECES - SLOTS)
        def _():
            pl.semaphore_signal(credit, inc=1, device_id=partner, device_id_type=MESH)

    def ln_send(stage):
        me, dev, n = ((core, None, 2), (tp, dev_x, 4), (y, dev_y, 4), (z, dev_z, 4))[stage]
        for d in range(1, n):
            to = partner if dev is None else dev(ring(me, d))
            remote(lnb.at[stage, me], lnb.at[stage, me], ln_s.at[stage], ln_r.at[stage], to).start()

    def ln_sum(stage):
        n = 2 if stage == 0 else 4
        ref = lnb.at[stage, pl.ds(0, n - 1)]
        drain(ref, ln_r.at[stage])
        drain(ref, ln_s.at[stage])
        if n == 2:
            return lnb[0, 0] + lnb[0, 1]
        return (lnb[stage, 0] + lnb[stage, 1]) + (lnb[stage, 2] + lnb[stage, 3])

    lnb[0, core] = lng_ref[...]

    @pl.loop(0, PIECES + 5)
    def _(p):
        @pl.when(p < PIECES)
        def _():
            compute(p)

        for lag, stage in ((5, stage_f2), (4, stage_l2), (3, stage_f1), (2, stage_l1), (1, stage_s)):
            @pl.when((p >= lag) & (p < PIECES + lag))
            def _():
                stage(p - lag)

        @pl.when(p == 0)
        def _():
            ln_send(0)
        for stage, me in ((1, tp), (2, y), (3, z)):
            @pl.when(p == stage)
            def _():
                lnb[stage, me] = ln_sum(stage - 1)
                ln_send(stage)

        @pl.when(p == 4)
        def _():
            o_ln[...] = ln_sum(3)

    for p in (PIECES - 2, PIECES - 1):
        drain(p_buf.at[p % 2, :, :, :, 0], ds.at[p])


def grads_call(gelu_out, dy_full, h_mlp, d_hidden, h_attn, d_proj, context, ln_part):
    hbm = pl.BlockSpec(memory_space=pl.ANY)
    vmem = pl.BlockSpec(memory_space=pltpu.VMEM)
    dma = pltpu.SemaphoreType.DMA
    tokens = 1024
    flops = 2 * tokens * 2048 * 512 * PIECES
    return pl.pallas_call(
        grads_kernel,
        out_shape=[jax.ShapeDtypeStruct((64, 2048), F32), jax.ShapeDtypeStruct((64, 2048), F32), jax.ShapeDtypeStruct((64, 1536), F32),
                   jax.ShapeDtypeStruct((16, 2048), F32), jax.ShapeDtypeStruct((8, 1024), F32)],
        in_specs=[hbm] * 7 + [vmem],
        out_specs=[vmem] * 5,
        scratch_shapes=[
            pltpu.VMEM((2, tokens, 2048), BF16),
            pltpu.VMEM((2, tokens, 512), BF16),
            pltpu.VMEM((2, 2, 4, 4, 2, 64, 256), F32),
            pltpu.VMEM((SLOTS, 2, 4, 4, 64, 256), F32),
            pltpu.VMEM((PIECES, 2, 2, 4, 32, 256), F32),
            pltpu.VMEM((PIECES, 2, 2, 2, 4, 32, 256), F32),
            pltpu.VMEM((PIECES, 2, 2, 32, 256), F32),
            pltpu.VMEM((PIECES, 2, 2, 2, 32, 256), F32),
            pltpu.VMEM((4, 4, 8, 1024), F32),
            dma((2,)), dma((2,)), dma((PIECES,)), dma((PIECES,)),
            dma((PIECES,)), dma((PIECES,)), dma((PIECES,)), dma((PIECES,)),
            dma((PIECES,)), dma((PIECES,)), dma((PIECES,)), dma((PIECES,)),
            dma((4,)), dma((4,)),
            pltpu.SemaphoreType.REGULAR,
        ],
        compiler_params=pltpu.CompilerParams(collective_id=0, has_side_effects=True, vmem_limit_bytes=64000 * 1024),
        cost_estimate=pl.CostEstimate(flops=flops * 4, bytes_accessed=100_000_000, transcendentals=0),
        name='weight_grads',
    )(gelu_out, dy_full, h_mlp, d_hidden, h_attn, d_proj, context, ln_part)


VMEM_LIMIT = 60000 * 1024


def whole(shape):
    return pl.BlockSpec(shape, lambda i: (0,) * len(shape), pipeline_mode=pl.Buffered(1))


def up_kernel(h_ref, w_ref, gelu_ref, slope_ref):
    @pl.loop(0, 4)
    def _(m):
        rows = pl.ds(pl.multiple_of(m * 256, 256), 256)
        u = dot_nn(h_ref[rows, :], w_ref[...]).astype(BF16).astype(F32)
        cdf = 0.5 * (1.0 + lax.erf(u * (0.5 ** 0.5)))
        gelu_ref[rows, :] = (u * cdf).astype(BF16)
        slope_ref[rows, :] = cdf + u * (jnp.exp(-0.5 * u * u) * ((2.0 * jnp.pi) ** -0.5))


def up_call(h_mlp, w_up):
    t, d = h_mlp.shape
    f, blk = w_up.shape[1], 256
    return pl.pallas_call(
        up_kernel,
        grid=(f // blk,),
        in_specs=[whole((t, d)), pl.BlockSpec((d, blk), lambda i: (0, i))],
        out_specs=[pl.BlockSpec((t, blk), lambda i: (0, i))] * 2,
        out_shape=[jax.ShapeDtypeStruct((t, f), BF16), jax.ShapeDtypeStruct((t, f), F32)],
        compiler_params=pltpu.CompilerParams(vmem_limit_bytes=VMEM_LIMIT),
        cost_estimate=pl.CostEstimate(flops=2 * t * d * f, bytes_accessed=2 * (t * d + d * f + 3 * t * f), transcendentals=2 * t * f),
        name='up',
    )(h_mlp, w_up)


def down_kernel(dy_ref, w_ref, slope_ref, out_ref):
    @pl.loop(0, 4)
    def _(m):
        rows = pl.ds(pl.multiple_of(m * 256, 256), 256)
        d_gelu = dot_nt(dy_ref[rows, :], w_ref[...]).astype(BF16).astype(F32)
        out_ref[rows, :] = (d_gelu * slope_ref[rows, :]).astype(BF16)


def down_call(dy_full, w_down, slope):
    t, d = dy_full.shape
    f, blk = w_down.shape[0], 256
    return pl.pallas_call(
        down_kernel,
        grid=(f // blk,),
        in_specs=[whole((t, d)), pl.BlockSpec((blk, d), lambda i: (i, 0)), pl.BlockSpec((t, blk), lambda i: (0, i))],
        out_specs=pl.BlockSpec((t, blk), lambda i: (0, i)),
        out_shape=jax.ShapeDtypeStruct((t, f), BF16),
        compiler_params=pltpu.CompilerParams(vmem_limit_bytes=VMEM_LIMIT),
        cost_estimate=pl.CostEstimate(flops=2 * t * d * f, bytes_accessed=2 * (t * d + d * f + 3 * t * f), transcendentals=0),
        name='down',
    )(dy_full, w_down, slope)


def attn_kernel(qkv_ref, dy_ref, w_ref, cos_ref, sin_ref, ctx_ref, dqkv_ref, q_s, k_s, dc_s, dk_s, dv_s):
    t, hd = ctx_ref.shape
    blk = 256
    scale = hd ** -0.5

    @pl.loop(0, t // blk)
    def _(m):
        rows = pl.ds(pl.multiple_of(m * blk, blk), blk)
        for i, dst in ((0, q_s), (1, k_s)):
            v = qkv_ref[rows, i * hd:(i + 1) * hd].astype(F32)
            dst[rows, :] = (v * cos_ref[rows, :] + pltpu.roll(v, hd // 2, 1) * sin_ref[rows, :]).astype(BF16)
        dc_s[rows, :] = dot_nt(dy_ref[rows, :], w_ref[...]).astype(BF16)

    def unrope(d, rows):
        d = d.astype(BF16).astype(F32)
        return (d * cos_ref[rows, :] - pltpu.roll(d, hd // 2, 1) * sin_ref[rows, :]).astype(BF16)

    for i in range(t // blk):
        rows, n = slice(i * blk, (i + 1) * blk), (i + 1) * blk
        qi, dci = q_s[rows, :], dc_s[rows, :]
        kn, vn = k_s[:n, :], qkv_ref[:n, 2 * hd:3 * hd]
        s = dot_nt(qi, kn) * scale
        row_id = lax.broadcasted_iota(jnp.int32, (blk, n), 0) + i * blk
        col_id = lax.broadcasted_iota(jnp.int32, (blk, n), 1)
        s = jnp.where(row_id >= col_id, s, -1e30)
        e = jnp.exp(s - jnp.max(s, axis=1, keepdims=True))
        p = e / jnp.sum(e, axis=1, keepdims=True)
        pb = p.astype(BF16)
        ctx_ref[rows, :] = dot_nn(pb, vn).astype(BF16)
        dp = dot_nt(dci, vn).astype(BF16).astype(F32)
        ds = p * (dp - jnp.sum(p * dp, axis=1, keepdims=True))
        dsb = (ds * scale).astype(BF16)
        dqkv_ref[rows, 0:hd] = unrope(dot_nn(dsb, kn), rows)
        dk, dv = dot_tt(dsb, qi), dot_tt(pb, dci)
        lo = n - blk
        dk_s[lo:n, :] = dk[lo:, :]
        dv_s[lo:n, :] = dv[lo:, :]
        if lo:
            dk_s[:lo, :] = dk_s[:lo, :] + dk[:lo, :]
            dv_s[:lo, :] = dv_s[:lo, :] + dv[:lo, :]

    @pl.loop(0, t // blk)
    def _(m):
        rows = pl.ds(pl.multiple_of(m * blk, blk), blk)
        dqkv_ref[rows, hd:2 * hd] = unrope(dk_s[rows, :], rows)
        dqkv_ref[rows, 2 * hd:3 * hd] = dv_s[rows, :].astype(BF16)


def attn_call(qkv, dy_full, w_out, cos_f, sin_f, hd):
    t, d = dy_full.shape
    heads = w_out.shape[0] // hd
    return pl.pallas_call(
        attn_kernel,
        grid=(heads,),
        in_specs=[pl.BlockSpec((t, 3 * hd), lambda i: (0, i)), whole((t, d)), pl.BlockSpec((hd, d), lambda i: (i, 0)),
                  whole((t, hd)), whole((t, hd))],
        out_specs=[pl.BlockSpec((t, hd), lambda i: (0, i)), pl.BlockSpec((t, 3 * hd), lambda i: (0, i))],
        out_shape=[jax.ShapeDtypeStruct((t, heads * hd), BF16), jax.ShapeDtypeStruct((t, 3 * heads * hd), BF16)],
        scratch_shapes=[pltpu.VMEM((t, hd), BF16)] * 3 + [pltpu.VMEM((t, hd), F32)] * 2,
        compiler_params=pltpu.CompilerParams(vmem_limit_bytes=VMEM_LIMIT),
        cost_estimate=pl.CostEstimate(flops=16_000_000_000, bytes_accessed=20_000_000, transcendentals=heads * t * t),
        name='attn',
    )(qkv, dy_full, w_out, cos_f, sin_f)


def inputs_kernel(dproj_ref, dhid_ref, wqkv_ref, wup_ref, x_ref, mean_ref, rstd_ref, ln_ref, c_ref, lng_ref):
    sums = []
    for m in range(4):
        rows = slice(m * 256, (m + 1) * 256)
        dha = dot_nt(dproj_ref[rows, :], wqkv_ref[...]).astype(BF16).astype(F32)
        dhm = dot_nt(dhid_ref[rows, :], wup_ref[...]).astype(BF16).astype(F32)
        x_hat = (x_ref[rows, :].astype(F32) - mean_ref[rows, :]) * rstd_ref[rows, :]
        c_ref[rows, :] = (dha * ln_ref[0:1, :] + dhm * ln_ref[2:3, :]).astype(BF16)
        sums.append([jnp.sum(v, axis=0, keepdims=True) for v in (dha * x_hat, dha, dhm * x_hat, dhm)])
    lng_ref[...] = jnp.concatenate([(sums[0][i] + sums[1][i]) + (sums[2][i] + sums[3][i]) for i in range(4)], axis=0)


def inputs_call(d_proj, d_hidden, w_qkv2, w_up, x_full, mean, rstd, ln_params):
    t, d = x_full.shape
    blk = 256
    n1, n2 = d_proj.shape[1], d_hidden.shape[1]
    return pl.pallas_call(
        inputs_kernel,
        grid=(d // blk,),
        in_specs=[whole((t, n1)), whole((t, n2)), pl.BlockSpec((blk, n1), lambda i: (i, 0)), pl.BlockSpec((blk, n2), lambda i: (i, 0)),
                  pl.BlockSpec((t, blk), lambda i: (0, i)), whole((t, 1)), whole((t, 1)), pl.BlockSpec((4, blk), lambda i: (0, i))],
        out_specs=[pl.BlockSpec((t, blk), lambda i: (0, i)), pl.BlockSpec((4, blk), lambda i: (0, i))],
        out_shape=[jax.ShapeDtypeStruct((t, d), BF16), jax.ShapeDtypeStruct((4, d), F32)],
        compiler_params=pltpu.CompilerParams(vmem_limit_bytes=VMEM_LIMIT),
        cost_estimate=pl.CostEstimate(flops=2 * t * d * (n1 + n2), bytes_accessed=30_000_000, transcendentals=0),
        name='inputs',
    )(d_proj, d_hidden, w_qkv2, w_up, x_full, mean, rstd, ln_params)


def solution(mesh):
    def local_step(x_loc, dy_loc, ln_params, w_qkv, w_out, w_up, w_down):
        x_full = lax.all_gather(x_loc, 'tp', axis=1, tiled=True)[0]
        dy_full = lax.all_gather(dy_loc, 'tp', axis=1, tiled=True)[0]
        seq_len, width = x_full.shape
        groups, slots, head_dim = w_qkv.shape[1:]

        def stats(rows):
            row_mean = jnp.mean(rows, axis=-1, keepdims=True)
            centered = rows - row_mean
            row_var = jnp.mean(centered * centered, axis=-1, keepdims=True)
            return row_mean, lax.rsqrt(row_var + NORM_EPS)

        x_f32 = x_full.astype(F32)
        mean, rstd = stats(x_f32)
        x_hat = (x_f32 - mean) * rstd
        h_attn = (x_hat * ln_params[0] + ln_params[1]).astype(BF16)
        h_mlp = (x_hat * ln_params[2] + ln_params[3]).astype(BF16)
        w_qkv2 = w_qkv.reshape(width, -1)
        qkv_proj = jnp.dot(h_attn, w_qkv2, preferred_element_type=F32).astype(BF16)
        cos_t, sin_t = rope_tables(jnp.arange(seq_len), head_dim)
        cos_f = jnp.concatenate([cos_t, cos_t], axis=1)
        sin_f = jnp.concatenate([-sin_t, sin_t], axis=1)
        gelu_out, slope = up_call(h_mlp, w_up)

        context, d_proj = attn_call(qkv_proj, dy_full, w_out, cos_f, sin_f, head_dim)
        d_hidden = down_call(dy_full, w_down, slope)
        c_part, ln_part = inputs_call(d_proj, d_hidden, w_qkv2, w_up, x_full, mean, rstd, ln_params)
        c_loc = lax.psum_scatter(c_part, 'tp', scatter_dimension=0, tiled=True)
        g_down, g_up, g_qkv, g_out, g_ln = grads_call(
            gelu_out, dy_full, h_mlp, d_hidden, h_attn, d_proj, context, ln_part.reshape(8, 1024))
        x_loc_f32 = x_loc[0].astype(F32)
        mean_loc, rstd_loc = stats(x_loc_f32)
        x_hat_loc = (x_loc_f32 - mean_loc) * rstd_loc
        c_loc = c_loc.astype(F32)
        dx = rstd_loc * (c_loc - jnp.mean(c_loc, -1, keepdims=True) - x_hat_loc * jnp.mean(c_loc * x_hat_loc, -1, keepdims=True))
        grad_x = (dy_loc[0].astype(F32) + dx).astype(BF16)[None]
        return grad_x, g_ln.reshape(4, width), g_qkv.reshape(64, groups, slots, head_dim), g_out, g_up, g_down

    act_spec = P('dp', 'tp', None)
    in_specs = (act_spec, act_spec, P(None, None), P(None, 'tp', None, None), P('tp', None), P(None, 'tp'), P('tp', None))
    out_specs = (act_spec, P(None, None), P('dp', 'tp', None, None), P(('tp', 'dp'), None), P('dp', 'tp'), P(('tp', 'dp'), None))
    return jax.shard_map(local_step, mesh=mesh, in_specs=in_specs, out_specs=out_specs, check_vma=False)
```

profile of v0, /device:TPU:0, one launch (start us, length us, event | category | flops | bytes accessed | tf_op | source)
XLA Modules:
  0.0 366.2 jit_solution(3630265178400999626)
XLA Ops:
  7.2 0.7 all-gather.3.cloned.1.call-update
  7.9 0.7 all-gather.5.cloned.1.call-update
  8.7 10.7 %copy.15 = bf16[2048,4,3,128]{0,3,2,1:T(8,128)(2,1)} copy(bf16[2048,4,3,128]{3,1,2,0:T(4,128)(2,1)} %param.10) | data formatting | bytes 12582912 | tf_op args[3]
  19.4 8.6 %copy.16.wqkv_ref = bf16[2048,1536]{1,0:T(8,128)(2,1)} copy(bf16[2048,1536]{0,1:T(8,128)(2,1)} %bitcast.51) | data formatting | bytes 12582912 | tf_op jit(solution)/shard_map/reshape | solution.py:514
  28.0 1.9 fusion.30
  29.9 1.3 pad_maximum_fusion
  31.2 0.2 convert_reduce_fusion.2
  31.4 0.4 fusion.27
  32.0 0.6 add_rsqrt_fusion.1
  32.6 27.6 %all-gather.3.cloned.1.call-done = bf16[1,1024,2048]{2,1,0:T(8,128)(2,1)} async-done(((bf16[1,256,2048]{2,1,0:T(8,128)(2,1)}), bf16[1,1024,2048]{2,1,0:T(8,128)(2,1)}) %all-gather.3.cloned.1.call-update) | async-done | bytes 4194320 | tf_op jit(solution)/shard_map/all_gather | solution.py:498
  60.2 3.0 convert_reduce_fusion
  63.2 0.5 copy-done
  63.6 1.2 fusion.8
  64.9 1.0 copy.18.rstd_ref
  65.9 1.0 copy.17.mean_ref
  67.0 6.3 %fusion.7 = (bf16[1024,2048]{1,0:T(8,128)(2,1)}, bf16[1024,2048]{1,0:T(8,128)(2,1)}) fusion(f32[2048]{0:T(1024)S(1)} %bitcast.55, f32[2048]{0:T(1024)S(1)} %bitcast.57, f32[1024]{0:T(1024)S(1)} %add_rsqrt_fusion, f32[1024]{0:T(1024)S(1)} %broadcast_multiply_fusion, bf16[1,1024,2048]{2,1,0:T(8,128)(2,1)} %all-gather.3.cloned.1.call-done, ...), kind=kLoop, calls=%fused_computation.9 | loop fusion | flops 18874368 | bytes 12623872 | tf_op jit(solution)/shard_map/convert_element_type | solution.py:512
  73.2 20.3 %up.1 = (bf16[1024,2048]{1,0:T(8,128)(2,1)}, f32[1024,2048]{1,0:T(8,128)}) custom-call(bf16[1024,2048]{1,0:T(8,128)(2,1)} %get-tuple-element.43.h_ref.hm_ref, bf16[2048,2048]{1,0:T(8,128)(2,1)} %wup_ref.1), custom_call_target="tpu_custom_call" | custom-call | flops 8589934592 | bytes 25165824 | tf_op jit(solution)/shard_map/up/pallas_call | solution.py:367
  93.5 16.8 %all-gather.5.cloned.1.call-done = bf16[1,1024,2048]{2,1,0:T(8,128)(2,1)} async-done(((bf16[1,256,2048]{2,1,0:T(8,128)(2,1)}), bf16[1,1024,2048]{2,1,0:T(8,128)(2,1)}) %all-gather.5.cloned.1.call-update) | async-done | bytes 4194320 | tf_op jit(solution)/shard_map/all_gather | solution.py:499
  110.3 19.5 %down.1.dhid_ref = bf16[1024,2048]{1,0:T(8,128)(2,1)} custom-call(bf16[1024,2048]{1,0:T(8,128)(2,1)} %bitcast.61, bf16[2048,2048]{1,0:T(8,128)(2,1)} %w_ref.5, f32[1024,2048]{1,0:T(8,128)} %get-tuple-element.18.slope_ref), custom_call_target="tpu_custom_call" | custom-call | flops 8589934592 | bytes 25165824 | tf_op jit(solution)/shard_map/down/pallas_call | solution.py:390
  129.9 11.0 %fusion.16.qkv_ref = bf16[1024,1536]{1,0:T(8,128)(2,1)} fusion(bf16[2048,1536]{0,1:T(8,128)(2,1)} %bitcast.52, bf16[1,1024,2048]{2,1,0:T(8,128)(2,1)S(1)} %copy-done.1, f32[2048]{0:T(1024)S(1)} %bitcast.56, f32[2048]{0:T(1024)S(1)} %bitcast.58, f32[1024]{0:T(1024)S(1)} %add_rsqrt_fusion, f32[1024]{0:T(1024)S(1)} %broadcast_multiply_fusion), kind=kOutput, calls=%fused_computation.18 | convolution fusion | flops 6456606720 | bytes 13656064 | tf_op jit(solution)/shard_map/dot_general | solution.py:515
  140.9 30.1 %attn.1 = (bf16[1024,512]{1,0:T(8,128)(2,1)}, bf16[1024,1536]{1,0:T(8,128)(2,1)}) custom-call(bf16[1024,1536]{1,0:T(8,128)(2,1)} %fusion.16.qkv_ref, bf16[1024,2048]{1,0:T(8,128)(2,1)} %bitcast.62, bf16[512,2048]{1,0:T(8,128)(2,1)} %w_ref.3, f32[1024,128]{1,0:T(8,128)} %get-tuple-element.51.cos_ref, f32[1024,128]{1,0:T(8,128)} %get-tuple-element.52.sin_ref), custom_call_target="tpu_custom_call" | custom-call | flops 16000000000 | bytes 20000000 | tf_op jit(solution)/shard_map/attn/pallas_call | solution.py:453
  171.0 23.7 %inputs.1 = (bf16[1024,2048]{1,0:T(8,128)(2,1)}, f32[4,2048]{1,0:T(4,128)}) custom-call(bf16[1024,1536]{1,0:T(8,128)(2,1)} %get-tuple-element.17.dproj_ref, bf16[1024,2048]{1,0:T(8,128)(2,1)} %down.1.dhid_ref, bf16[2048,1536]{1,0:T(8,128)(2,1)} %copy.16.wqkv_ref, bf16[2048,2048]{1,0:T(8,128)(2,1)} %wup_ref.1, bf16[1024,2048]{1,0:T(8,128)(2,1)} %bitcast.50, ...), custom_call_target="tpu_custom_call" | custom-call | flops 15032385536 | bytes 30000000 | tf_op jit(solution)/shard_map/inputs/pallas_call | solution.py:483
  194.6 1.4 reshape.115.lng_ref
  196.1 151.5 %weight_grads.1 = (f32[64,2048]{1,0:T(8,128)}, f32[64,2048]{1,0:T(8,128)}, f32[64,1536]{1,0:T(8,128)}, f32[16,2048]{1,0:T(8,128)}, f32[8,1024]{1,0:T(8,128)}) custom-call(bf16[1024,2048]{1,0:T(8,128)(2,1)} %get-tuple-element.20.gelu_ref, bf16[1024,2048]{1,0:T(8,128)(2,1)} %bitcast.63, bf16[1024,2048]{1,0:T(8,128)(2,1)} %get-tuple-element.43.h_ref.hm_ref, ...), custom_call_target="tpu_custom_call" | custom-call | flops 103079215104 | bytes 100000000 | tf_op jit(solution)/shard_map/weight_grads/pallas_call | solution.py:319
  347.6 1.4 reshape.117
  349.0 0.8 copy.19
  349.8 1.4 reshape.116
  351.3 1.9 convert_reduce_fusion.1
  353.2 3.1 fusion.29
  356.3 0.7 copy.23
  357.0 1.9 copy.24
  358.8 0.8 copy.25
  (34 shorter events, 0.4 us)
Async XLA Ops:
  7.2 53.0 %all-gather.3.cloned.1.call-start = ((), (), s32[]{:S(2)}) async-start(), calls=%async_computation.1 | async-start | bytes 5242880 | tf_op jit(solution)/shard_map/all_gather | solution.py:498
  7.9 102.4 %all-gather.5.cloned.1.call-start = ((), (), s32[]{:S(2)}) async-start(), calls=%async_computation.2 | async-start | bytes 5242880 | tf_op jit(solution)/shard_map/all_gather | solution.py:499
  8.6 342.6 %reduce-scatter.2.cloned.1.call-start = ((), (), s32[]{:S(2)}) async-start(), calls=%async_computation.3 | async-start | bytes 5242880 | tf_op jit(solution)/shard_map/reduce_scatter | solution.py:524
  27.9 3.2 copy-start.2
  27.9 4.7 %copy-start.7 = (f32[4,2048]{1,0:T(4,128)S(1)}, f32[4,2048]{1,0:T(4,128)}, u32[]{:S(2)}) copy-start(f32[4,2048]{1,0:T(4,128)} %ln_ref.1) | copy-start | bytes 98308
  31.4 0.6 copy-start.8
  60.2 3.4 copy-start
  110.3 19.5 %copy-start.1 = (bf16[1,1024,2048]{2,1,0:T(8,128)(2,1)S(1)}, bf16[1,1024,2048]{2,1,0:T(8,128)(2,1)}, u32[]{:S(2)}) copy-start(bf16[1,1024,2048]{2,1,0:T(8,128)(2,1)} %all-gather.3.cloned.1.call-done) | copy-start | bytes 12582916
  196.0 155.2 %copy-start.3 = (bf16[1,256,2048]{2,1,0:T(8,128)(2,1)S(1)}, bf16[1,256,2048]{2,1,0:T(8,128)(2,1)}, u32[]{:S(2)}) copy-start(bf16[1,256,2048]{2,1,0:T(8,128)(2,1)} %param.7) | copy-start | bytes 3145732
  196.1 155.2 %copy-start.9 = (f32[256]{0:T(256)S(1)}, f32[256]{0:T(256)}, u32[]{:S(2)}) copy-start(f32[256]{0:T(256)} %copy-done.8) | copy-start | bytes 3076
  196.1 155.2 %copy-start.10 = (f32[256]{0:T(256)S(1)}, f32[256]{0:T(256)}, u32[]{:S(2)}) copy-start(f32[256]{0:T(256)} %add_rsqrt_fusion.1) | copy-start | bytes 3076
  347.6 5.6 %copy-start.4 = (bf16[1,256,2048]{2,1,0:T(8,128)(2,1)S(1)}, bf16[1,256,2048]{2,1,0:T(8,128)(2,1)}, u32[]{:S(2)}) copy-start(bf16[1,256,2048]{2,1,0:T(8,128)(2,1)} %param.8) | copy-start | bytes 3145732
  347.6 8.7 %copy-start.6 = (f32[16,2048]{1,0:T(8,128)S(1)}, f32[16,2048]{1,0:T(8,128)}, u32[]{:S(2)}) copy-start(f32[16,2048]{1,0:T(8,128)} %get-tuple-element.62) | copy-start | bytes 393220
  349.8 9.0 %copy-start.5 = (f32[64,2048]{1,0:T(8,128)S(1)}, f32[64,2048]{1,0:T(8,128)}, u32[]{:S(2)}) copy-start(f32[64,2048]{1,0:T(8,128)} %get-tuple-element.64) | copy-start | bytes 1572868
Sparse Core Ops, SparseCore 0:
  9.6 50.5 all-gather.2
  61.8 48.4 all-gather.4
  196.2 48.6 reduce-scatter.1
where the time goes:
time: 367 us; the launch traced here: 366 us
  Pallas kernels  245 us (67%)
  waiting for transfers between devices  45.8 us (12%)
  local copies, waits for them, and re-layouts  30.4 us (8%)
  other arithmetic  19.9 us (5%)
  between operations  13.9 us (4%)
  matrix products  11 us (3%)
    pallas_call x1, Pallas kernels, grads_call(): pl.pallas_call(grads_kernel, out_shape=[jax.ShapeDtypeStruct((64, 2048),...  151 us
    pallas_call x1, Pallas kernels, attn_call(): pl.pallas_call(attn_kernel, grid=(heads,), in_specs=[pl.BlockSpec((t, 3 *...  30.1 us
    all_gather x1, waiting for transfers between devices, local_step(): x_full = lax.all_gather(x_loc, 'tp', axis=1, tiled=True)[0]  27.6 us
    pallas_call x1, Pallas kernels, inputs_call(): pl.pallas_call(inputs_kernel, grid=(d // blk,), in_specs=[whole((t, n1)),...  23.7 us
    pallas_call x1, Pallas kernels, up_call(): pl.pallas_call(up_kernel, grid=(f // blk,), in_specs=[whole((t, d)), pl.B...  20.3 us
    pallas_call x1, Pallas kernels, down_call(): pl.pallas_call(down_kernel, grid=(f // blk,), in_specs=[whole((t, d)), pl...  19.5 us
    all_gather x1, waiting for transfers between devices, local_step(): dy_full = lax.all_gather(dy_loc, 'tp', axis=1, tiled=True)[0]  16.8 us
    unnamed x27, local copies, waits for them, and re-layouts  15.5 us
  transfers between devices with their start and end apart: 3, of which 2 were waited for; matrix products, arithmetic and copies ran while one was open for 11% of the time, Pallas kernels for 47%

commit v1 on v0

--- a/solution.py
+++ b/solution.py
@@ -2,6 +2,7 @@
 
 import jax
 import jax.numpy as jnp
+import numpy as np
 from jax import lax
 from jax.experimental import pallas as pl
 from jax.experimental.pallas import tpu as pltpu
@@ -16,11 +17,12 @@
 BF16 = jnp.bfloat16
 
 
-def rope_tables(positions, head_dim):
+def rope_tables(seq_len, head_dim):
     half_dim = head_dim // 2
-    inv_freq = ROPE_BASE ** (-2.0 * jnp.arange(half_dim, dtype=jnp.float32) / head_dim)
-    angles = positions.astype(jnp.float32)[:, None] * inv_freq[None, :]
-    return jnp.cos(angles), jnp.sin(angles)
+    inv_freq = np.float32(ROPE_BASE) ** (np.float32(-2.0) * np.arange(half_dim, dtype=np.float32) / np.float32(head_dim))
+    angles = np.arange(seq_len, dtype=np.float32)[:, None] * inv_freq[None, :].astype(np.float32)
+    cos_t, sin_t = np.cos(angles), np.sin(angles)
+    return np.concatenate([cos_t, cos_t], axis=1), np.concatenate([-sin_t, sin_t], axis=1)
 
 
 def dot_nn(lhs, rhs):
@@ -319,7 +321,7 @@
     return pl.pallas_call(
         grads_kernel,
         out_shape=[jax.ShapeDtypeStruct((64, 2048), F32), jax.ShapeDtypeStruct((64, 2048), F32), jax.ShapeDtypeStruct((64, 1536), F32),
-                   jax.ShapeDtypeStruct((16, 2048), F32), jax.ShapeDtypeStruct((8, 1024), F32)],
+                   jax.ShapeDtypeStruct((16, 2048), F32), jax.ShapeDtypeStruct((4, 2048), F32)],
         in_specs=[hbm] * 7 + [vmem],
         out_specs=[vmem] * 5,
         scratch_shapes=[
@@ -331,7 +333,7 @@
             pltpu.VMEM((PIECES, 2, 2, 2, 4, 32, 256), F32),
             pltpu.VMEM((PIECES, 2, 2, 32, 256), F32),
             pltpu.VMEM((PIECES, 2, 2, 2, 32, 256), F32),
-            pltpu.VMEM((4, 4, 8, 1024), F32),
+            pltpu.VMEM((4, 4, 4, 2048), F32),
             dma((2,)), dma((2,)), dma((PIECES,)), dma((PIECES,)),
             dma((PIECES,)), dma((PIECES,)), dma((PIECES,)), dma((PIECES,)),
             dma((PIECES,)), dma((PIECES,)), dma((PIECES,)), dma((PIECES,)),
@@ -351,52 +353,212 @@
     return pl.BlockSpec(shape, lambda i: (0,) * len(shape), pipeline_mode=pl.Buffered(1))
 
 
-def up_kernel(h_ref, w_ref, gelu_ref, slope_ref):
-    @pl.loop(0, 4)
-    def _(m):
-        rows = pl.ds(pl.multiple_of(m * 256, 256), 256)
-        u = dot_nn(h_ref[rows, :], w_ref[...]).astype(BF16).astype(F32)
-        cdf = 0.5 * (1.0 + lax.erf(u * (0.5 ** 0.5)))
-        gelu_ref[rows, :] = (u * cdf).astype(BF16)
-        slope_ref[rows, :] = cdf + u * (jnp.exp(-0.5 * u * u) * ((2.0 * jnp.pi) ** -0.5))
-
-
-def up_call(h_mlp, w_up):
-    t, d = h_mlp.shape
-    f, blk = w_up.shape[1], 256
+def front_kernel(x_ref, dy_ref, ln_ref, wq_ref, wu_ref, wd_ref,
+                 o_x, o_dy, o_ha, o_hm, o_qkv, o_gelu, o_dhid, o_w, mean_ref, rstd_ref,
+                 x_v, dy_v, w2, wu, wd, wq_b, wq_f, slope, ha, hm, qkv, ge, dh,
+                 xs, xr, ds, dr, in_sem, wq_sem, out_sem, fin_sem):
+    tp = lax.axis_index('tp')
+    nxt, opp, prv = lax.rem(tp + 1, 4), lax.rem(tp + 2, 4), lax.rem(tp + 3, 4)
+    d_model = x_ref.shape[1]
+    rows = x_ref.shape[0]
+    half = rows // 2
+    part = wq_b.shape[1]
+    barrier = pltpu.get_barrier_semaphore()
+    for peer in (nxt, prv):
+        pl.semaphore_signal(barrier, inc=1, device_id={'tp': peer}, device_id_type=MESH)
+
+    def wq_copy(i):
+        return pltpu.make_async_copy(wq_ref.at[pl.ds(i * part, part)], wq_b.at[i % 2], wq_sem.at[i % 2])
+
+    loads = [pltpu.make_async_copy(x_ref, x_v.at[tp], in_sem.at[0]), pltpu.make_async_copy(dy_ref, dy_v.at[tp], in_sem.at[1]),
+             pltpu.make_async_copy(wu_ref, wu, in_sem.at[2]), pltpu.make_async_copy(wd_ref, wd, in_sem.at[3])]
+    wq_copy(0).start()
+    loads[0].start()
+    wq_copy(1).start()
+    loads[2].start()
+    loads[1].start()
+    loads[3].start()
+    pl.semaphore_wait(barrier, 2)
+
+    A, B = pl.ds(0, half), pl.ds(half, half)
+
+    def moves(src, buf, ssem, rsem):
+        def one(i, ref, slot, piece, to):
+            return pltpu.make_async_remote_copy(src_ref=ref, dst_ref=buf.at[slot, piece], send_sem=ssem.at[i], recv_sem=rsem.at[i],
+                                                device_id={'tp': to}, device_id_type=MESH)
+        return [one(0, src.at[A], tp, A, nxt), one(1, src.at[B], tp, B, prv), one(2, src.at[B], tp, B, nxt), one(3, src.at[A], tp, A, prv),
+                one(4, buf.at[prv, A], prv, A, nxt), one(5, buf.at[nxt, B], nxt, B, prv)]
+
+    xm = moves(x_ref, x_v, xs, xr)
+    dm = moves(dy_ref, dy_v, ds, dr)
+    for i in range(4):
+        xm[i].start()
+
+    per = part // 12
+    for i in range(wq_ref.shape[0] // part):
+        wq_copy(i).wait()
+
+        @pl.loop(0, part // 256)
+        def _(r):
+            at = pl.ds(pl.multiple_of(r * 256, 256), 256)
+            wq_f[at, :] = wq_b[i % 2, at, :].astype(F32)
+
+        if i + 2 < wq_ref.shape[0] // part:
+            wq_copy(i + 2).start()
+        for j in range(3):
+            for g in range(4):
+                w2[i * per:(i + 1) * per, g * 384 + j * 128:g * 384 + j * 128 + 128] = wq_f[pl.ds(j * 4 + g, per, stride=12), :].astype(BF16)
+    w_out_copy = pltpu.make_async_copy(w2, o_w, fin_sem.at[8])
+    w_out_copy.start()
+
+    outs = {}
+
+    def put(kind, n, buf, ref, slot):
+        copy = pltpu.make_async_copy(buf.at[n % 2], ref.at[pl.ds(pl.multiple_of(slot * rows, rows), rows)], out_sem.at[kind, n % 2])
+        copy.start()
+        outs[kind, n % 2] = copy
+
+    def free(kind, n):
+        if (kind, n % 2) in outs:
+            outs.pop((kind, n % 2)).wait()
+
+    def forward(slot, n):
+        s = n % 2
+        base = slot * rows
+        for kind in range(4):
+            free(kind, n)
+
+        @pl.loop(0, rows // 32)
+        def _(r):
+            at = pl.ds(pl.multiple_of(r * 32, 32), 32)
+            to = pl.ds(pl.multiple_of(base + r * 32, 32), 32)
+            xf = x_v[slot, at, :].astype(F32)
+            mean = jnp.mean(xf, axis=-1, keepdims=True)
+            cen = xf - mean
+            rstd = lax.rsqrt(jnp.mean(cen * cen, axis=-1, keepdims=True) + NORM_EPS)
+            mean_ref[to, :] = mean
+            rstd_ref[to, :] = rstd
+            x_hat = cen * rstd
+            ha[s, at, :] = (x_hat * ln_ref[0:1, :] + ln_ref[1:2, :]).astype(BF16)
+            hm[s, at, :] = (x_hat * ln_ref[2:3, :] + ln_ref[3:4, :]).astype(BF16)
+
+        put(0, n, ha, o_ha, slot)
+        put(1, n, hm, o_hm, slot)
+
+        @pl.loop(0, 3)
+        def _(c):
+            cols = pl.ds(pl.multiple_of(c * 512, 512), 512)
+            qkv[s, :, cols] = dot_nn(ha[s], w2[:, cols]).astype(BF16)
+
+        put(2, n, qkv, o_qkv, slot)
+
+    def up(slot, n):
+        s = n % 2
+
+        @pl.loop(0, 4)
+        def _(c):
+            cols = pl.ds(pl.multiple_of(c * 512, 512), 512)
+            u = dot_nn(hm[s], wu[:, cols]).astype(BF16).astype(F32)
+            cdf = 0.5 * (1.0 + lax.erf(u * (0.5 ** 0.5)))
+            ge[s, :, cols] = (u * cdf).astype(BF16)
+            slope[slot, :, cols] = cdf + u * (jnp.exp(-0.5 * u * u) * ((2.0 * jnp.pi) ** -0.5))
+
+        put(3, n, ge, o_gelu, slot)
+
+    def down(slot, n):
+        s = n % 2
+        free(4, n)
+
+        @pl.loop(0, 4)
+        def _(c):
+            cols = pl.ds(pl.multiple_of(c * 512, 512), 512)
+            d_gelu = dot_nt(dy_v[slot], wd[cols, :]).astype(BF16).astype(F32)
+            dh[s, :, cols] = (d_gelu * slope[slot, :, cols]).astype(BF16)
+
+        put(4, n, dh, o_dhid, slot)
+
+    fins = []
+
+    def keep(buf, ref, slot, i):
+        copy = pltpu.make_async_copy(buf.at[slot], ref.at[pl.ds(pl.multiple_of(slot * rows, rows), rows)], fin_sem.at[i])
+        copy.start()
+        fins.append(copy)
+
+    loads[0].wait()
+    forward(tp, 0)
+    loads[2].wait()
+    up(tp, 0)
+    keep(x_v, o_x, tp, 0)
+    xm[0].wait_recv()
+    xm[4].start()
+    xm[1].wait_recv()
+    xm[5].start()
+    for i in range(4):
+        dm[i].start()
+    loads[1].wait()
+    loads[3].wait()
+    down(tp, 0)
+    keep(dy_v, o_dy, tp, 4)
+    xm[2].wait_recv()
+    forward(prv, 1)
+    up(prv, 1)
+    keep(x_v, o_x, prv, 1)
+    xm[3].wait_recv()
+    forward(nxt, 2)
+    up(nxt, 2)
+    keep(x_v, o_x, nxt, 2)
+    dm[0].wait_recv()
+    dm[4].start()
+    dm[1].wait_recv()
+    dm[5].start()
+    xm[4].wait_recv()
+    xm[5].wait_recv()
+    forward(opp, 3)
+    up(opp, 3)
+    keep(x_v, o_x, opp, 3)
+    dm[2].wait_recv()
+    down(prv, 1)
+    keep(dy_v, o_dy, prv, 5)
+    dm[3].wait_recv()
+    down(nxt, 2)
+    keep(dy_v, o_dy, nxt, 6)
+    dm[4].wait_recv()
+    dm[5].wait_recv()
+    down(opp, 3)
+    keep(dy_v, o_dy, opp, 7)
+    for m in xm + dm:
+        m.wait_send()
+    for copy in list(outs.values()) + fins + [w_out_copy]:
+        copy.wait()
+
+
+def front_call(x_loc, dy_loc, ln_params, w_rows, w_up, w_down):
+    r, d = x_loc.shape
+    t, f, n = 4 * r, w_up.shape[1], w_rows.shape[0] * 128 // d
+    part = w_rows.shape[0] // 4
+    hbm = pl.BlockSpec(memory_space=pl.ANY)
+    vmem = pl.BlockSpec(memory_space=pltpu.VMEM)
+    dma = pltpu.SemaphoreType.DMA
+    shape = jax.ShapeDtypeStruct
     return pl.pallas_call(
-        up_kernel,
-        grid=(f // blk,),
-        in_specs=[whole((t, d)), pl.BlockSpec((d, blk), lambda i: (0, i))],
-        out_specs=[pl.BlockSpec((t, blk), lambda i: (0, i))] * 2,
-        out_shape=[jax.ShapeDtypeStruct((t, f), BF16), jax.ShapeDtypeStruct((t, f), F32)],
-        compiler_params=pltpu.CompilerParams(vmem_limit_bytes=VMEM_LIMIT),
-        cost_estimate=pl.CostEstimate(flops=2 * t * d * f, bytes_accessed=2 * (t * d + d * f + 3 * t * f), transcendentals=2 * t * f),
-        name='up',
-    )(h_mlp, w_up)
-
-
-def down_kernel(dy_ref, w_ref, slope_ref, out_ref):
-    @pl.loop(0, 4)
-    def _(m):
-        rows = pl.ds(pl.multiple_of(m * 256, 256), 256)
-        d_gelu = dot_nt(dy_ref[rows, :], w_ref[...]).astype(BF16).astype(F32)
-        out_ref[rows, :] = (d_gelu * slope_ref[rows, :]).astype(BF16)
-
-
-def down_call(dy_full, w_down, slope):
-    t, d = dy_full.shape
-    f, blk = w_down.shape[0], 256
-    return pl.pallas_call(
-        down_kernel,
-        grid=(f // blk,),
-        in_specs=[whole((t, d)), pl.BlockSpec((blk, d), lambda i: (i, 0)), pl.BlockSpec((t, blk), lambda i: (0, i))],
-        out_specs=pl.BlockSpec((t, blk), lambda i: (0, i)),
-        out_shape=jax.ShapeDtypeStruct((t, f), BF16),
-        compiler_params=pltpu.CompilerParams(vmem_limit_bytes=VMEM_LIMIT),
-        cost_estimate=pl.CostEstimate(flops=2 * t * d * f, bytes_accessed=2 * (t * d + d * f + 3 * t * f), transcendentals=0),
-        name='down',
-    )(dy_full, w_down, slope)
+        front_kernel,
+        in_specs=[hbm, hbm, vmem, hbm, hbm, hbm],
+        out_specs=[hbm] * 8 + [vmem] * 2,
+        out_shape=[shape((t, d), BF16)] * 4 + [shape((t, n), BF16), shape((t, f), BF16), shape((t, f), BF16), shape((d, n), BF16),
+                                               shape((t, 1), F32), shape((t, 1), F32)],
+        scratch_shapes=[
+            pltpu.VMEM((4, r, d), BF16), pltpu.VMEM((4, r, d), BF16),
+            pltpu.VMEM((d, n), BF16), pltpu.VMEM((d, f), BF16), pltpu.VMEM((f, d), BF16),
+            pltpu.VMEM((2, part, 128), BF16), pltpu.VMEM((part, 128), F32),
+            pltpu.VMEM((4, r, f), F32),
+            pltpu.VMEM((2, r, d), BF16), pltpu.VMEM((2, r, d), BF16), pltpu.VMEM((2, r, n), BF16),
+            pltpu.VMEM((2, r, f), BF16), pltpu.VMEM((2, r, f), BF16),
+            dma((6,)), dma((6,)), dma((6,)), dma((6,)), dma((4,)), dma((2,)), dma((5, 2)), dma((9,)),
+        ],
+        compiler_params=pltpu.CompilerParams(collective_id=1, has_side_effects=True, vmem_limit_bytes=64000 * 1024),
+        cost_estimate=pl.CostEstimate(flops=2 * t * d * (n + 2 * f), bytes_accessed=70_000_000, transcendentals=2 * t * f),
+        name='front',
+    )(x_loc, dy_loc, ln_params, w_rows, w_up, w_down)
 
 
 def attn_kernel(qkv_ref, dy_ref, w_ref, cos_ref, sin_ref, ctx_ref, dqkv_ref, q_s, k_s, dc_s, dk_s, dv_s):
@@ -465,15 +627,12 @@
 
 
 def inputs_kernel(dproj_ref, dhid_ref, wqkv_ref, wup_ref, x_ref, mean_ref, rstd_ref, ln_ref, c_ref, lng_ref):
-    sums = []
-    for m in range(4):
-        rows = slice(m * 256, (m + 1) * 256)
-        dha = dot_nt(dproj_ref[rows, :], wqkv_ref[...]).astype(BF16).astype(F32)
-        dhm = dot_nt(dhid_ref[rows, :], wup_ref[...]).astype(BF16).astype(F32)
-        x_hat = (x_ref[rows, :].astype(F32) - mean_ref[rows, :]) * rstd_ref[rows, :]
-        c_ref[rows, :] = (dha * ln_ref[0:1, :] + dhm * ln_ref[2:3, :]).astype(BF16)
-        sums.append([jnp.sum(v, axis=0, keepdims=True) for v in (dha * x_hat, dha, dhm * x_hat, dhm)])
-    lng_ref[...] = jnp.concatenate([(sums[0][i] + sums[1][i]) + (sums[2][i] + sums[3][i]) for i in range(4)], axis=0)
+    dha = dot_nt(dproj_ref[...], wqkv_ref[...]).astype(BF16).astype(F32)
+    dhm = dot_nt(dhid_ref[...], wup_ref[...]).astype(BF16).astype(F32)
+    x_hat = (x_ref[...].astype(F32) - mean_ref[...]) * rstd_ref[...]
+    c_ref[...] = (dha * ln_ref[0:1, :] + dhm * ln_ref[2:3, :]).astype(BF16)
+    sums = [jnp.sum(v, axis=0, keepdims=True) for v in (dha * x_hat, dha, dhm * x_hat, dhm)]
+    lng_ref[...] = jnp.concatenate(sums, axis=0)
 
 
 def inputs_call(d_proj, d_hidden, w_qkv2, w_up, x_full, mean, rstd, ln_params):
@@ -495,10 +654,8 @@
 
 def solution(mesh):
     def local_step(x_loc, dy_loc, ln_params, w_qkv, w_out, w_up, w_down):
-        x_full = lax.all_gather(x_loc, 'tp', axis=1, tiled=True)[0]
-        dy_full = lax.all_gather(dy_loc, 'tp', axis=1, tiled=True)[0]
-        seq_len, width = x_full.shape
-        groups, slots, head_dim = w_qkv.shape[1:]
+        width, groups, slots, head_dim = w_qkv.shape
+        seq_len = 4 * x_loc.shape[1]
 
         def stats(rows):
             row_mean = jnp.mean(rows, axis=-1, keepdims=True)
@@ -506,31 +663,22 @@
             row_var = jnp.mean(centered * centered, axis=-1, keepdims=True)
             return row_mean, lax.rsqrt(row_var + NORM_EPS)
 
-        x_f32 = x_full.astype(F32)
-        mean, rstd = stats(x_f32)
-        x_hat = (x_f32 - mean) * rstd
-        h_attn = (x_hat * ln_params[0] + ln_params[1]).astype(BF16)
-        h_mlp = (x_hat * ln_params[2] + ln_params[3]).astype(BF16)
-        w_qkv2 = w_qkv.reshape(width, -1)
-        qkv_proj = jnp.dot(h_attn, w_qkv2, preferred_element_type=F32).astype(BF16)
-        cos_t, sin_t = rope_tables(jnp.arange(seq_len), head_dim)
-        cos_f = jnp.concatenate([cos_t, cos_t], axis=1)
-        sin_f = jnp.concatenate([-sin_t, sin_t], axis=1)
-        gelu_out, slope = up_call(h_mlp, w_up)
-
-        context, d_proj = attn_call(qkv_proj, dy_full, w_out, cos_f, sin_f, head_dim)
-        d_hidden = down_call(dy_full, w_down, slope)
+        w_rows = w_qkv.transpose(0, 2, 1, 3).reshape(width * slots * groups, head_dim)
+        x_full, dy_full, h_attn, h_mlp, qkv_proj, gelu_out, d_hidden, w_qkv2, mean, rstd = front_call(
+            x_loc[0], dy_loc[0], ln_params, w_rows, w_up, w_down)
+        cos_f, sin_f = rope_tables(seq_len, head_dim)
+        context, d_proj = attn_call(qkv_proj, dy_full, w_out, jnp.asarray(cos_f), jnp.asarray(sin_f), head_dim)
         c_part, ln_part = inputs_call(d_proj, d_hidden, w_qkv2, w_up, x_full, mean, rstd, ln_params)
         c_loc = lax.psum_scatter(c_part, 'tp', scatter_dimension=0, tiled=True)
         g_down, g_up, g_qkv, g_out, g_ln = grads_call(
-            gelu_out, dy_full, h_mlp, d_hidden, h_attn, d_proj, context, ln_part.reshape(8, 1024))
+            gelu_out, dy_full, h_mlp, d_hidden, h_attn, d_proj, context, ln_part)
         x_loc_f32 = x_loc[0].astype(F32)
         mean_loc, rstd_loc = stats(x_loc_f32)
         x_hat_loc = (x_loc_f32 - mean_loc) * rstd_loc
         c_loc = c_loc.astype(F32)
         dx = rstd_loc * (c_loc - jnp.mean(c_loc, -1, keepdims=True) - x_hat_loc * jnp.mean(c_loc * x_hat_loc, -1, keepdims=True))
         grad_x = (dy_loc[0].astype(F32) + dx).astype(BF16)[None]
-        return grad_x, g_ln.reshape(4, width), g_qkv.reshape(64, groups, slots, head_dim), g_out, g_up, g_down
+        return grad_x, g_ln, g_qkv.reshape(64, groups, slots, head_dim), g_out, g_up, g_down
 
     act_spec = P('dp', 'tp', None)
     in_specs = (act_spec, act_spec, P(None, None), P(None, 'tp', None, None), P('tp', None), P(None, 'tp'), P('tp', None))

time: 367 us -> 308 us (0.84)
  waiting for transfers between devices: 45.8 us -> 0.04 us
  Pallas kernels: 245 us -> 284 us
  local copies, waits for them, and re-layouts: 30.4 us -> 5.1 us
  other arithmetic: 19.9 us -> 4.55 us
  matrix products: 11 us -> 0 us
    all_gather x2 -> x0, waiting for transfers between devices: 44.4 us -> none  [the longest x1 27.6 us: local_step(): x_full = lax.all_gather(x_loc, 'tp', axis=1, tiled=True)[0]]
    pallas_call x2 -> x1, Pallas kernels: 39.8 us -> 77.8 us  [front_call(): pl.pallas_call(front_kernel, in_specs=[hbm, hbm, vmem, hbm, hbm, hbm], ou...]
    unnamed x27 -> x19, local copies, waits for them, and re-layouts: 15.5 us -> 3.74 us
    reshape x3 -> x0, local copies, waits for them, and re-layouts: 11.4 us -> none  [the longest x1 8.59 us: local_step(): w_qkv2 = w_qkv.reshape(width, -1)]
    dot_general x1 -> x0, matrix products: 11 us -> none  [local_step(): qkv_proj = jnp.dot(h_attn, w_qkv2, preferred_element_type=F32).astype(BF16)]
    convert_element_type x2 -> x0, other arithmetic: 6.27 us -> none  [the longest x1 6.27 us: local_step(): h_attn = (x_hat * ln_params[0] + ln_params[1]).astype(BF16)]
  transfers between devices with their start and end apart: 3 -> 1, of which waited for: 2 -> 0; matrix products, arithmetic and copies ran while one was open for 11% -> 1% of each run, Pallas kernels for 47% -> 50%
where the time goes in v1:
time: 308 us; the launch traced here: 307 us
  Pallas kernels  284 us (92%)
  between operations  14.1 us (5%)
  local copies, waits for them, and re-layouts  5.1 us (2%)
  other arithmetic  4.55 us (1%)
    pallas_call x1, Pallas kernels, grads_call(): pl.pallas_call(grads_kernel, out_shape=[jax.ShapeDtypeStruct((64, 2048),...  153 us
    pallas_call x1, Pallas kernels, front_call(): pl.pallas_call(front_kernel, in_specs=[hbm, hbm, vmem, hbm, hbm, hbm], ou...  77.8 us
    pallas_call x1, Pallas kernels, attn_call(): pl.pallas_call(attn_kernel, grid=(heads,), in_specs=[pl.BlockSpec((t, 3 *...  30.3 us
    pallas_call x1, Pallas kernels, inputs_call(): pl.pallas_call(inputs_kernel, grid=(d // blk,), in_specs=[whole((t, n1)),...  22.8 us
  transfers between devices with their start and end apart: 1, of which 0 were waited for; matrix products, arithmetic and copies ran while one was open for 1% of the time, Pallas kernels for 50%

profile of v1, /device:TPU:0, one launch (start us, length us, event | category | flops | bytes accessed | tf_op | source)
XLA Modules:
  0.0 307.5 jit_solution(10145238494869111099)
XLA Ops:
  7.2 0.0 reduce-scatter.2.cloned.1.call-start
  7.2 77.8 %front.1 = (bf16[1024,2048]{1,0:T(8,128)(2,1)}, bf16[1024,2048]{1,0:T(8,128)(2,1)}, bf16[1024,2048]{1,0:T(8,128)(2,1)}, bf16[1024,2048]{1,0:T(8,128)(2,1)}, bf16...) custom-call(bf16[256,2048]{1,0:T(8,128)(2,1)} %bitcast.12, ...), custom_call_target="tpu_custom_call" | custom-call | flops 23622320128 | bytes 70000000 | tf_op jit(solution)/shard_map/front/pallas_call | solution.py:543
  85.0 30.3 %attn.1 = (bf16[1024,512]{1,0:T(8,128)(2,1)}, bf16[1024,1536]{1,0:T(8,128)(2,1)}) custom-call(bf16[1024,1536]{1,0:T(8,128)(2,1)} %get-tuple-element.25.qkv_ref, bf16[1024,2048]{1,0:T(8,128)(2,1)} %get-tuple-element.26.dy_ref, bf16[512,2048]{1,0:T(8,128)(2,1)} %w_ref.1, f32[1024,128]{1,0:T(8,128)} %constant.14.clone.cos_ref, f32[1024,128]{1,0:T(8,128)} %constant.15.clone.sin_ref), custom_call_target="tpu_custom_call" | custom-call | flops 16000000000 | bytes 20000000 | tf_op jit(solution)/shard_map/attn/pallas_call | solution.py:615
  115.4 22.8 %inputs.1 = (bf16[1024,2048]{1,0:T(8,128)(2,1)}, f32[4,2048]{1,0:T(4,128)}) custom-call(bf16[1024,1536]{1,0:T(8,128)(2,1)} %get-tuple-element.27.dproj_ref, bf16[1024,2048]{1,0:T(8,128)(2,1)} %get-tuple-element.28.dhid_ref, bf16[2048,1536]{1,0:T(8,128)(2,1)} %get-tuple-element.29.wqkv_ref, bf16[2048,2048]{1,0:T(8,128)(2,1)} %wup_ref.1, ...), custom_call_target="tpu_custom_call" | custom-call | flops 15032385536 | bytes 30000000 | tf_op jit(solution)/shard_map/inputs/pallas_call | solution.py:642
  138.2 0.0 reduce-scatter.2.cloned.1.call-update
  138.2 152.6 %weight_grads.1 = (f32[64,2048]{1,0:T(8,128)}, f32[64,2048]{1,0:T(8,128)}, f32[64,1536]{1,0:T(8,128)}, f32[16,2048]{1,0:T(8,128)}, f32[4,2048]{1,0:T(4,128)}) custom-call(bf16[1024,2048]{1,0:T(8,128)(2,1)} %get-tuple-element.34.gelu_ref, bf16[1024,2048]{1,0:T(8,128)(2,1)} %get-tuple-element.26.dy_ref, bf16[1024,2048]{1,0:T(8,128)(2,1)} %get-tuple-element.35.hm_ref, ...), custom_call_target="tpu_custom_call" | custom-call | flops 103079215104 | bytes 100000000 | tf_op jit(solution)/shard_map/weight_grads/pallas_call | solution.py:321
  290.8 0.0 copy-start
  290.9 1.4 reshape.39
  292.2 0.8 copy.16
  293.1 0.0 copy-done
  293.1 0.0 copy-start.2
  293.1 0.2 convert_reduce_fusion.1
  293.3 0.4 fusion.7
  293.7 0.0 reduce-scatter.2.cloned.1.call-done
  293.8 0.0 copy-start.1
  293.8 2.0 convert_reduce_fusion
  295.8 0.0 copy-done.2
  295.8 0.0 copy-done.1
  295.8 0.0 copy-start.6
  295.8 0.0 copy-start.5
  295.8 0.0 copy-start.4
  295.8 0.0 copy-start.3
  295.9 1.9 fusion.9
  297.7 0.0 copy-done.6
  297.7 0.6 copy.21
  298.4 0.0 copy-done.5
  298.4 0.7 copy.22
  299.0 0.0 copy-done.4
  299.0 0.8 copy.23
  299.8 0.0 copy-done.3
  299.8 0.8 copy.24
  (3 shorter events, 0.0 us)
Async XLA Ops:
  7.2 286.6 %reduce-scatter.2.cloned.1.call-start = ((), (), s32[]{:S(2)}) async-start(), calls=%async_computation.1 | async-start | bytes 5242880 | tf_op jit(solution)/shard_map/reduce_scatter | solution.py:672
  290.8 2.2 copy-start
  293.1 2.7 copy-start.2
  293.8 2.0 copy-start.1
  295.8 1.9 copy-start.6
  295.8 2.5 copy-start.5
  295.8 3.2 %copy-start.4 = (f32[64,2048]{1,0:T(8,128)S(1)}, f32[64,2048]{1,0:T(8,128)}, u32[]{:S(2)}) copy-start(f32[64,2048]{1,0:T(8,128)} %get-tuple-element.70) | copy-start | bytes 1572868
  295.8 4.0 %copy-start.3 = (f32[64,2048]{1,0:T(8,128)S(1)}, f32[64,2048]{1,0:T(8,128)}, u32[]{:S(2)}) copy-start(f32[64,2048]{1,0:T(8,128)} %get-tuple-element.71) | copy-start | bytes 1572868
Sparse Core Ops, SparseCore 0:
  138.3 49.9 reduce-scatter.1
